TPU v7x, 32 devices: a whole 2x2x4 slice. The times are simulated.
32 devices in a mesh: groups: 2 (over x), tm: 8 (over z, y), tile: 2 (over core).
Axes of the slice: x: 2, y: 2, z: 4, core: 2. Of those that a mesh axis runs over, the one named last changes fastest.
Arguments:
- movie: bfloat16 [4, 2304, 4096], P(('groups', 'tile'), None, 'tm'), parts along dimension 0, may hold values from 0 to 4
- cycle_weights: bfloat16 [4, 2304, 56], P(('groups', 'tile')), parts along dimension 0, may hold values from -0.75 to 0.75
- footprints: bfloat16 [4, 2304, 384], P(('groups', 'tile')), parts along dimension 0, may hold values from 0.19921875 to 1
- traces: bfloat16 [4, 384, 4096], P(('groups', 'tile'), None, 'tm'), parts along dimension 0, may hold values from 0 to 1.5
- centre_row: int32 [4, 384], P(('groups', 'tile')), parts along dimension 0, may hold values from 0 to 47
- centre_col: int32 [4, 384], P(('groups', 'tile')), parts along dimension 0, may hold values from 0 to 47
- radius: int32 [4, 384], P(('groups', 'tile')), parts along dimension 0, may hold values from 4 to 9
- comp_count: int32 [4], P(('groups', 'tile')), parts along dimension 0, may hold values from 64 to 384
Outputs:
- new_footprints: bfloat16 [4, 2304, 384], P(('groups', 'tile')), parts along dimension 0
- new_traces: bfloat16 [4, 384, 4096], P(('groups', 'tile'), None, 'tm'), parts along dimension 0
There are 2 independent parts, one for each index of `groups`. A program takes and returns all parts, laid end to end along the dimension named above; each array names one. Nothing has to cross between parts.
All inputs are finite; a program needn't handle non-finite values.
Results may differ from a plain program's by a relative error of at most 0.0034.
Values may be sent and summed in bfloat16 or wider, within the bound.
A program may use at most 64 MiB of HBM per device.

v0:
```python
import functools

import jax
import jax.numpy as jnp
import numpy as np
from jax import lax
from jax.experimental import pallas as pl
from jax.experimental.pallas import tpu as pltpu
from jax.sharding import PartitionSpec as P

SIDE = 48
CYCLE = 8
WIDE = SIDE + 2 * CYCLE
FOLD_ROWS = 16
FOLD = 24
HALF = FOLD // 2
PASSES = 2
RIDGE_TERM = 1.0
BLOCK = 8
DEPTH = 16
SPAN = BLOCK + 2 * CYCLE
LANES = 128
F32 = jnp.float32
BF16 = jnp.bfloat16
MESH = pl.DeviceIdType.MESH


def cycle_offsets():
    found = []
    for row_step in range(-CYCLE, CYCLE + 1):
        for col_step in range(-CYCLE, CYCLE + 1):
            dist_sq = row_step * row_step + col_step * col_step
            if CYCLE * CYCLE <= dist_sq < (CYCLE + 1) * (CYCLE + 1):
                found.append((row_step, col_step))
    return found


def spread_tables():
    offsets = cycle_offsets()
    width = WIDE * (2 * CYCLE + 2)
    tables = np.zeros((2, len(offsets), width), np.float32)
    for index, (row_step, col_step) in enumerate(offsets):
        for odd in range(2):
            tables[odd, index, (row_step + CYCLE + odd) * WIDE + col_step + CYCLE] = 1.0
    return tables


def swap_halves(rows):
    return jnp.concatenate([rows[:, HALF:], rows[:, :HALF]], axis=1)


def fold(rows, s):
    rows = rows[:, :FOLD] + rows[:, FOLD:]
    rows = rows[:s] + swap_halves(rows[s : 2 * s]) + rows[2 * s :]
    return rows.reshape(s * FOLD, rows.shape[2])


def kernel(
    n, s, shares,
    movie, stored, prints, traces, row_at, col_at, reach, count, tables,
    new_foot, new_trace,
    feet_edge, seen_edge, weights, foot, band, pm, win, errs, backs, trace, gacc, inv_den, col_sq,
    halo_out, halo_in, part, own, arrived, energy_out, energy_in, gathered,
    halo_sems, part_sems, energy_sems, gather_sems,
):
    me = lax.axis_index("tm")
    tile = lax.axis_index("tile")
    frames = movie.shape[2]
    comps = prints.shape[2]
    blocks = SIDE // BLOCK

    barrier = pltpu.get_barrier_semaphore()
    pl.semaphore_signal(barrier, inc=1, device_id={"tile": 1 - tile}, device_id_type=MESH)

    def greet(t, carry):
        peer = lax.rem(me + 1 + t, n)
        pl.semaphore_signal(barrier, inc=1, device_id={"tm": peer}, device_id_type=MESH)
        return carry

    lax.fori_loop(0, n - 1, greet, 0)

    live_row = lax.broadcasted_iota(jnp.int32, (1, comps), 1) < count[0]
    bound = jnp.where(live_row, reach[...] * reach[...], -1)
    col_gap = lax.broadcasted_iota(jnp.int32, (SIDE, comps), 0) - col_at[...]
    col_sq[...] = col_gap * col_gap

    def mask_row(r, total):
        row_gap = r - row_at[...]
        keep = col_sq[...] <= bound - row_gap * row_gap
        kept = jnp.where(keep, prints[r].astype(F32), 0.0)
        foot[r] = kept.astype(BF16)
        return total + kept * kept

    total = lax.fori_loop(0, SIDE, mask_row, jnp.zeros((SIDE, comps), F32))
    den = jnp.sum(total, axis=0, keepdims=True) + RIDGE_TERM
    inv_den[...] = jnp.transpose(jnp.broadcast_to(1.0 / den, (LANES, comps)))
    live = lax.broadcasted_iota(jnp.int32, (comps, LANES), 0) < count[0]
    for q in range(frames // LANES):
        cols = slice(q * LANES, (q + 1) * LANES)
        trace[:, cols] = jnp.where(live, traces[:, cols].astype(F32), 0.0).astype(BF16)

    def cut_edge(j, carry):
        rows = pl.ds(j * DEPTH, DEPTH)
        spots = pl.ds(j * DEPTH * CYCLE, DEPTH * CYCLE)
        for ref, edge in ((foot, feet_edge), (movie, seen_edge)):
            whole = ref[rows].astype(F32)
            cut = jnp.where(tile == 0, whole[:, SIDE - CYCLE :], whole[:, :CYCLE])
            edge[spots] = cut.reshape(DEPTH * CYCLE, ref.shape[2]).astype(BF16)
        return carry

    lax.fori_loop(0, SIDE // DEPTH, cut_edge, 0)
    pixels = BLOCK * SIDE
    for b in range(blocks):
        turned = jnp.transpose(stored[:, b * pixels : (b + 1) * pixels].astype(F32))
        weights[b * BLOCK : (b + 1) * BLOCK] = turned.astype(BF16).reshape(BLOCK, SIDE, -1)
    pl.semaphore_wait(barrier, n)

    def halo_copy(sweep):
        return pltpu.make_async_remote_copy(
            src_ref=halo_out.at[sweep],
            dst_ref=halo_in.at[sweep],
            send_sem=halo_sems.at[0, sweep],
            recv_sem=halo_sems.at[1, sweep],
            device_id={"tile": 1 - tile},
            device_id_type=MESH,
        )

    def build_band(b, carry):
        for i in range(BLOCK):
            spread = jnp.dot(weights[b * BLOCK + i], tables[i % 2], preferred_element_type=F32)
            first = (i // 2) * LANES
            rows = slice(i * SIDE, (i + 1) * SIDE)
            if first > 0:
                band[b, rows, 0:first] = jnp.zeros((SIDE, first), BF16)
            for q in range(spread.shape[1] // LANES):
                skewed = pltpu.roll(
                    spread[:, q * LANES : (q + 1) * LANES], 0, 1, stride=1, stride_axis=0
                )
                band[b, rows, first + q * LANES : first + (q + 1) * LANES] = skewed.astype(BF16)
            last = first + spread.shape[1]
            if last < SPAN * WIDE:
                band[b, rows, last:] = jnp.zeros((SIDE, SPAN * WIDE - last), BF16)
        return carry

    for sweep in range(PASSES):

        def residual(b, carry):
            rows = pl.ds(b * DEPTH, DEPTH)
            prod = jnp.dot(
                foot[rows].reshape(DEPTH * SIDE, comps), trace[...], preferred_element_type=F32
            )
            diff = prod.reshape(DEPTH, SIDE, frames) - movie[rows].astype(F32)
            pm[rows] = diff
            return carry

        ahead = jnp.dot(feet_edge[...], trace[...], preferred_element_type=F32)
        halo_out[sweep] = (seen_edge[...].astype(F32) - ahead).astype(BF16)
        copy = halo_copy(sweep)
        copy.start()
        lax.fori_loop(0, SIDE // DEPTH, residual, 0)
        if sweep == 0:
            lax.fori_loop(0, blocks, build_band, 0)
        copy.wait_recv()

        def fill(b, carry):
            rows = pl.ds(b * BLOCK, BLOCK)
            edge = halo_in[sweep, pl.ds(b * BLOCK * CYCLE, BLOCK * CYCLE)]
            edge = edge.astype(F32).reshape(BLOCK, CYCLE, frames)
            low = jnp.where(tile == 0, 0.0, edge)
            high = jnp.where(tile == 0, edge, 0.0)
            whole = jnp.concatenate([low, -pm[rows], high], axis=1)
            win[rows] = whole.astype(BF16)
            return carry

        lax.fori_loop(0, blocks, fill, 0)

        for b in range(blocks):
            rows = slice(b * BLOCK, (b + 1) * BLOCK)
            first = b * BLOCK - CYCLE
            low, high = max(first, 0), min(first + SPAN, SIDE)
            seen = win[low:high].reshape((high - low) * WIDE, frames)
            taps = band[b, :, (low - first) * WIDE : (high - first) * WIDE]
            back = jnp.dot(taps, seen, preferred_element_type=F32).astype(BF16)
            back = back.reshape(BLOCK, SIDE, frames)
            if sweep == PASSES - 1:
                backs[rows] = back
            errs[rows] = (pm[rows] + back.astype(F32)).astype(BF16)

        gacc[...] = jnp.zeros_like(gacc)

        def descend(j, carry):
            rows = pl.ds(j * DEPTH, DEPTH)
            gacc[...] += lax.dot_general(
                foot[rows].reshape(DEPTH * SIDE, comps),
                errs[rows].reshape(DEPTH * SIDE, frames),
                (((0,), (0,)), ((), ())),
                preferred_element_type=F32,
            )
            return carry

        lax.fori_loop(0, SIDE // DEPTH, descend, 0)
        for q in range(frames // LANES):
            cols = slice(q * LANES, (q + 1) * LANES)
            moved = jnp.maximum(trace[:, cols].astype(F32) - gacc[:, cols] * inv_den[...], 0.0)
            trace[:, cols] = jnp.where(live, moved, 0.0).astype(BF16)

    new_trace[...] = trace[...]
    squares = jnp.zeros((comps, LANES), F32)
    for q in range(frames // LANES):
        now = trace[:, q * LANES : (q + 1) * LANES].astype(F32)
        squares = squares + now * now
    energy = jnp.sum(jnp.transpose(squares), axis=0, keepdims=True)
    energy_out[...] = jnp.broadcast_to(energy, energy_out.shape)

    def energy_copy(peer, sender):
        return pltpu.make_async_remote_copy(
            src_ref=energy_out,
            dst_ref=energy_in.at[sender],
            send_sem=energy_sems.at[0, peer],
            recv_sem=energy_sems.at[1, sender],
            device_id={"tm": peer},
            device_id_type=MESH,
        )

    def part_copy(peer, sender):
        return pltpu.make_async_remote_copy(
            src_ref=part.at[peer],
            dst_ref=arrived.at[sender],
            send_sem=part_sems.at[0, peer],
            recv_sem=part_sems.at[1, sender],
            device_id={"tm": peer},
            device_id_type=MESH,
        )

    def gather_copy(peer, sender):
        return pltpu.make_async_remote_copy(
            src_ref=gathered.at[sender],
            dst_ref=gathered.at[sender],
            send_sem=gather_sems.at[0, peer],
            recv_sem=gather_sems.at[1, sender],
            device_id={"tm": peer},
            device_id_type=MESH,
        )

    def owns(index, do):
        if shares == n:
            do()
        else:
            pl.when(index < shares)(do)

    def over_peers(do):
        def step(t, carry):
            do(lax.rem(me + 1 + t, n))
            return carry

        lax.fori_loop(0, n - 1, step, 0)

    over_peers(lambda peer: owns(peer, lambda: energy_copy(peer, me).start()))

    def rows_of(ref, share):
        return [ref[pl.ds(a * FOLD_ROWS + share * s, s)] for a in range(SIDE // FOLD_ROWS)]

    def share_of(share):
        held = SIDE // FOLD_ROWS * s * SIDE
        feet = jnp.concatenate(rows_of(foot, share), axis=0).reshape(held, comps)
        prod = jnp.dot(feet, trace[...], preferred_element_type=F32)
        back = jnp.concatenate(rows_of(backs, share), axis=0).reshape(held, frames)
        seen = jnp.concatenate(rows_of(movie, share), axis=0).reshape(held, frames)
        ferr = (prod + back.astype(F32) - seen.astype(F32)).astype(BF16)
        grad = lax.dot_general(
            ferr, trace[...], (((1,), (1,)), ((), ())), preferred_element_type=F32
        )
        grad = jnp.where(feet.astype(F32) > 0.0, grad, 0.0)
        return fold(grad.reshape(held // SIDE, SIDE, comps), s)

    def send_share(share):
        part[share] = share_of(share).astype(BF16)
        part_copy(share, me).start()

    over_peers(lambda peer: owns(peer, lambda: send_share(peer)))

    def settle():
        own[...] = share_of(me)
        energy_in[me] = energy_out[...]

        def take(peer):
            energy_copy(me, peer).wait_recv()
            part_copy(me, peer).wait_recv()
            own[...] += arrived[peer].astype(F32)
            energy_in[me] += energy_in[peer]

        over_peers(take)
        den_c = energy_in[me][:1] + RIDGE_TERM
        feet = fold(jnp.concatenate(rows_of(foot, me), axis=0).astype(F32), s)
        gathered[me] = jnp.maximum(feet - own[...] / den_c, 0.0).astype(BF16)
        over_peers(lambda peer: gather_copy(peer, me).start())

    owns(me, settle)

    def unfold(share):
        values = gathered[share].astype(F32).reshape(s, FOLD, comps)
        turned = swap_halves(values)
        values = jnp.concatenate([values, values], axis=1)
        turned = jnp.concatenate([turned, turned], axis=1)
        for a in range(SIDE // FOLD_ROWS):
            rows = pl.ds(a * FOLD_ROWS + share * s, s)
            new_foot[rows] = jnp.where(foot[rows].astype(F32) > 0.0, (values, turned)[a % 2], 0.0).astype(BF16)

    owns(me, lambda: unfold(me))

    def receive(peer):
        gather_copy(me, peer).wait_recv()
        unfold(peer)

    over_peers(lambda peer: owns(peer, lambda: receive(peer)))

    for sweep in range(PASSES):
        halo_copy(sweep).wait_send()

    def drain(peer):
        owns(peer, lambda: energy_copy(peer, me).wait_send())
        owns(peer, lambda: part_copy(peer, me).wait_send())
        owns(me, lambda: gather_copy(peer, me).wait_send())

    over_peers(drain)


def shards(movie, cycle_weights, footprints, traces, centre_row, centre_col, radius, comp_count):
    n = lax.axis_size("tm")
    frames = movie.shape[2]
    comps = footprints.shape[2]
    s = -(-FOLD_ROWS // n)
    while FOLD_ROWS % s:
        s += 1
    shares = FOLD_ROWS // s
    blocks = SIDE // BLOCK
    tables = jnp.asarray(spread_tables(), BF16)
    vmem = pl.BlockSpec(memory_space=pltpu.VMEM)
    smem = pl.BlockSpec(memory_space=pltpu.SMEM)
    new_foot, new_trace = pl.pallas_call(
        functools.partial(kernel, n, s, shares),
        out_shape=(
            jax.ShapeDtypeStruct((SIDE, SIDE, comps), BF16),
            jax.ShapeDtypeStruct((comps, frames), BF16),
        ),
        in_specs=[vmem] * 7 + [smem, vmem],
        out_specs=(vmem, vmem),
        scratch_shapes=[
            pltpu.VMEM((SIDE * CYCLE, comps), BF16),
            pltpu.VMEM((SIDE * CYCLE, frames), BF16),
            pltpu.VMEM((SIDE, SIDE, cycle_weights.shape[2]), BF16),
            pltpu.VMEM((SIDE, SIDE, comps), BF16),
            pltpu.VMEM((blocks, BLOCK * SIDE, SPAN * WIDE), BF16),
            pltpu.VMEM((SIDE, SIDE, frames), F32),
            pltpu.VMEM((SIDE, WIDE, frames), BF16),
            pltpu.VMEM((SIDE, SIDE, frames), BF16),
            pltpu.VMEM((SIDE, SIDE, frames), BF16),
            pltpu.VMEM((comps, frames), BF16),
            pltpu.VMEM((comps, frames), F32),
            pltpu.VMEM((comps, LANES), F32),
            pltpu.VMEM((SIDE, comps), jnp.int32),
            pltpu.VMEM((PASSES, SIDE * CYCLE, frames), BF16),
            pltpu.VMEM((PASSES, SIDE * CYCLE, frames), BF16),
            pltpu.VMEM((n, s * FOLD, comps), BF16),
            pltpu.VMEM((s * FOLD, comps), F32),
            pltpu.VMEM((n, s * FOLD, comps), BF16),
            pltpu.VMEM((8, comps), F32),
            pltpu.VMEM((n, 8, comps), F32),
            pltpu.VMEM((n, s * FOLD, comps), BF16),
            pltpu.SemaphoreType.DMA((2, PASSES)),
            pltpu.SemaphoreType.DMA((2, n)),
            pltpu.SemaphoreType.DMA((2, n)),
            pltpu.SemaphoreType.DMA((2, n)),
        ],
        compiler_params=pltpu.CompilerParams(
            collective_id=0, has_side_effects=True, vmem_limit_bytes=60 * 1024 * 1024
        ),
    )(
        movie.reshape(SIDE, SIDE, frames),
        jnp.transpose(cycle_weights[0]),
        footprints.reshape(SIDE, SIDE, comps),
        traces.reshape(comps, frames),
        centre_row,
        centre_col,
        radius,
        comp_count,
        tables,
    )
    return (new_foot.reshape(1, SIDE * SIDE, comps), new_trace[None])


def solution(mesh):
    in_specs = (
        P(("groups", "tile"), None, "tm"),
        P(("groups", "tile"), None, None),
        P(("groups", "tile"), None, None),
        P(("groups", "tile"), None, "tm"),
        P(("groups", "tile"), None),
        P(("groups", "tile"), None),
        P(("groups", "tile"), None),
        P(("groups", "tile")),
    )
    out_specs = (P(("groups", "tile"), None, None), P(("groups", "tile"), None, "tm"))
    return jax.shard_map(shards, mesh=mesh, in_specs=in_specs, out_specs=out_specs, check_vma=False)
```

profile of v0, /device:TPU:0, one launch (start us, length us, event | category | flops | bytes accessed | tf_op | source)
XLA Modules:
  0.0 49.4 jit_solution(12698685167578294875)
XLA Ops:
  1.3 44.5 %shard_map.104 = (bf16[48,48,384]{2,1,0:T(8,128)(2,1)}, bf16[384,512]{1,0:T(8,128)(2,1)}) custom-call(bf16[48,48,512]{2,1,0:T(8,128)(2,1)} %bitcast.8, bf16[56,2304]{1,0:T(8,128)(2,1)} %bitcast.13, bf16[48,48,384]{2,1,0:T(8,128)(2,1)} %bitcast.9, bf16[384,512]{1,0:T(8,128)(2,1)} %bitcast.11, s32[1,384]{1,0:T(1,128)} %row_at.1, s32[1,384]{1,0:T(1,128)} %col_at.1, ...), custom_call_target="tpu_custom_call" | custom-call | tf_op jit(solution)/shard_map/pallas_call | solution.py:340
  45.8 0.0 copy-start
  45.8 2.9 %copy.14 = bf16[1,2304,384]{2,1,0:T(8,128)(2,1)} copy(bf16[1,2304,384]{2,1,0:T(8,128)(2,1)} %bitcast.10) | data formatting | bytes 3538944
  48.7 0.0 copy-done
  48.7 0.7 %copy.15 = bf16[1,384,512]{2,1,0:T(8,128)(2,1)} copy(bf16[1,384,512]{2,1,0:T(8,128)(2,1)S(1)} %bitcast.12) | data formatting | bytes 786432
Async XLA Ops:
  45.8 2.9 %copy-start = (bf16[384,512]{1,0:T(8,128)(2,1)S(1)}, bf16[384,512]{1,0:T(8,128)(2,1)}, u32[]{:S(2)}) copy-start(bf16[384,512]{1,0:T(8,128)(2,1)} %get-tuple-element.5) | copy-start | bytes 1179652
where the time goes:
time: 49.6 us; the launch traced here: 49.4 us
  Pallas kernels  44.5 us (90%)
  local copies, waits for them, and re-layouts  3.66 us (7%)
  between operations  1.3 us (3%)
    pallas_call x1, Pallas kernels, shards(): pl.pallas_call(functools.partial(kernel, n, s, shares), out_shape=(jax.Sh...  44.5 us
    unnamed x4, local copies, waits for them, and re-layouts  3.66 us

commit v1 on v0

v1 whole, which is shorter than its diff:
```python
import functools

import jax
import jax.numpy as jnp
import numpy as np
from jax import lax
from jax.experimental import pallas as pl
from jax.experimental.pallas import tpu as pltpu
from jax.sharding import PartitionSpec as P

SIDE = 48
CYCLE = 8
PASSES = 2
RIDGE_TERM = 1.0
EDGE = 16
TILES = SIDE // EDGE
SPAN = EDGE + 2 * CYCLE
LANES = 128
STEP = LANES // SPAN
CHUNKS = (STEP - 1 + 2 * CYCLE) // STEP + 1
FOLD_ROWS = 24
SHIFT = FOLD_ROWS // 2
F32 = jnp.float32
BF16 = jnp.bfloat16
MESH = pl.DeviceIdType.MESH


def cycle_offsets():
    found = []
    for row_step in range(-CYCLE, CYCLE + 1):
        for col_step in range(-CYCLE, CYCLE + 1):
            dist_sq = row_step * row_step + col_step * col_step
            if CYCLE * CYCLE <= dist_sq < (CYCLE + 1) * (CYCLE + 1):
                found.append((row_step, col_step))
    return found


def tap_tables():
    offsets = {step: index for index, step in enumerate(cycle_offsets())}
    tables = np.full((STEP, CHUNKS, EDGE, LANES), len(offsets), np.int32)
    for phase in range(STEP):
        for chunk in range(CHUNKS):
            for col in range(EDGE):
                for lane in range(LANES):
                    row_step = chunk * STEP + lane // SPAN - phase - CYCLE
                    col_step = lane % SPAN - col - CYCLE
                    if (row_step, col_step) in offsets:
                        tables[phase, chunk, col, lane] = offsets[(row_step, col_step)]
    return tables


def kernel(
    n, s, shares,
    movie_in, stored_in, prints_in, traces_in, row_in, col_in, reach_in, count, tables_in,
    packed, new_trace,
    movie, stored, prints, trace, row_at, col_at, reach, tables,
    weights, foot, band, pm, win, errs, backs, inv_den,
    halo_out, halo_in, part, own, arrived, energy_out, energy_in, gathered,
    load_sems, small_sems, halo_sems, part_sems, energy_sems, gather_sems, out_sems,
):
    me = lax.axis_index("tm")
    tile = lax.axis_index("tile")
    frames = movie.shape[3]
    comps = foot.shape[3]
    pixels = SIDE * SIDE

    def load(b, j, kind):
        source, target = ((prints_in, prints), (movie_in, movie))[kind]
        rows = slice(b * EDGE, (b + 1) * EDGE)
        return pltpu.make_async_copy(
            source.at[rows, j * EDGE : (j + 1) * EDGE], target.at[j, rows], load_sems.at[kind, b, j]
        )

    smalls = [
        pltpu.make_async_copy(source, target, small_sems.at[index])
        for index, (source, target) in enumerate((
            (row_in, row_at), (col_in, col_at), (reach_in, reach),
            (stored_in, stored), (tables_in, tables), (traces_in, trace),
        ))
    ]
    for copy in smalls:
        copy.start()
    for b in range(TILES):
        for kind in range(2):
            for j in range(TILES):
                load(b, j, kind).start()

    barrier = pltpu.get_barrier_semaphore()
    pl.semaphore_signal(barrier, inc=1, device_id={"tile": 1 - tile}, device_id_type=MESH)

    def greet(t, carry):
        peer = lax.rem(me + 1 + t, n)
        pl.semaphore_signal(barrier, inc=1, device_id={"tm": peer}, device_id_type=MESH)
        return carry

    lax.fori_loop(0, n - 1, greet, 0)

    blank = jnp.zeros((SIDE, CYCLE, frames), BF16)
    for sweep in range(PASSES):
        win[sweep, :, 0, 0:CYCLE] = blank
        win[sweep, :, TILES, CYCLE:EDGE] = blank

    for copy in smalls:
        copy.wait()
    live_row = lax.broadcasted_iota(jnp.int32, (1, comps), 1) < count[0]
    bound = jnp.where(live_row, reach[...] * reach[...], -1)
    live = lax.broadcasted_iota(jnp.int32, (comps, LANES), 0) < count[0]
    for q in range(frames // LANES):
        cols = slice(q * LANES, (q + 1) * LANES)
        trace[:, cols] = jnp.where(live, trace[:, cols].astype(F32), 0.0).astype(BF16)

    taps = stored.shape[0]
    run = CYCLE * SIDE
    for b in range(SIDE // CYCLE):
        values = stored[:, b * run : (b + 1) * run].astype(F32)
        values = jnp.concatenate([values, jnp.zeros((LANES - taps, run), F32)], axis=0)
        weights[b * CYCLE : (b + 1) * CYCLE] = jnp.transpose(values).reshape(CYCLE, TILES, EDGE, LANES)

    col_sq = []
    for j in range(TILES):
        gap = lax.broadcasted_iota(jnp.int32, (EDGE, comps), 0) + j * EDGE - col_at[...]
        col_sq.append(gap * gap)

    def store_window(sweep, rows, j, diff):
        resid = (-diff).astype(BF16)
        win[sweep, rows, j, CYCLE:EDGE] = resid[:, 0:CYCLE]
        win[sweep, rows, j + 1, 0:CYCLE] = resid[:, CYCLE:EDGE]

    def opening(b):
        def step(q, total):
            for phase in range(STEP):
                r = b * EDGE + q * STEP + phase
                spot = pl.multiple_of((q * STEP + phase) * EDGE, EDGE)
                row_gap = r - row_at[...]
                edge = bound - row_gap * row_gap
                for j in range(TILES):
                    kept = jnp.where(col_sq[j] <= edge, prints[j, r].astype(F32), 0.0)
                    foot[j, r] = kept.astype(BF16)
                    total = total + kept * kept
                    held = weights[r, j]
                    for chunk in range(CHUNKS):
                        found = [
                            jnp.take_along_axis(
                                held[h * 8 : h * 8 + 8], tables[phase, chunk, h * 8 : h * 8 + 8], axis=1
                            )
                            for h in range(EDGE // 8)
                        ]
                        lane = pl.multiple_of((q + chunk) * LANES, LANES)
                        band[j, b, pl.ds(spot, EDGE), pl.ds(lane, LANES)] = jnp.concatenate(found, axis=0).astype(BF16)
                    for chunk in range(CHUNKS, SPAN // STEP):
                        lane = pl.multiple_of(lax.rem(q + chunk, SPAN // STEP) * LANES, LANES)
                        band[j, b, pl.ds(spot, EDGE), pl.ds(lane, LANES)] = jnp.zeros((EDGE, LANES), BF16)
            rows = pl.ds(b * EDGE + q * STEP, STEP)
            feet = foot[:, rows].reshape(TILES * STEP * EDGE, comps)
            prod = jnp.dot(feet, trace[...], preferred_element_type=F32)
            prod = prod.reshape(TILES, STEP, EDGE, frames)
            for j in range(TILES):
                diff = prod[j] - movie[j, rows].astype(F32)
                pm[j, rows] = diff
                store_window(0, rows, j, diff)
            return total

        return step

    total = jnp.zeros((EDGE, comps), F32)
    for b in range(TILES):
        for kind in range(2):
            for j in range(TILES):
                load(b, j, kind).wait()
        total = lax.fori_loop(0, EDGE // STEP, opening(b), total)
    den = jnp.sum(total, axis=0, keepdims=True) + RIDGE_TERM
    inv_den[...] = jnp.transpose(jnp.broadcast_to(1.0 / den, (LANES, comps)))

    def halo_copy(sweep):
        return pltpu.make_async_remote_copy(
            src_ref=halo_out.at[sweep],
            dst_ref=halo_in.at[sweep],
            send_sem=halo_sems.at[0, sweep],
            recv_sem=halo_sems.at[1, sweep],
            device_id={"tile": 1 - tile},
            device_id_type=MESH,
        )

    def send_halo(sweep, diff):
        cut = jnp.where(tile == 0, diff[:, CYCLE:EDGE], diff[:, 0:CYCLE])
        halo_out[sweep] = (-cut).reshape(SIDE * CYCLE, frames).astype(BF16)
        halo_copy(sweep).start()

    near = [jnp.where(tile == 0, TILES - 1 - t, t) for t in range(TILES)]
    for sweep in range(PASSES):
        if sweep == 0:
            pl.semaphore_wait(barrier, n)
            send_halo(0, pm[near[0]])
        else:
            for t in range(TILES):
                j = near[t]
                prod = jnp.dot(
                    foot[j].reshape(SIDE * EDGE, comps), trace[...], preferred_element_type=F32
                )
                diff = prod.reshape(SIDE, EDGE, frames) - movie[j].astype(F32)
                pm[j] = diff
                store_window(sweep, slice(0, SIDE), j, diff)
                if t == 0:
                    send_halo(sweep, diff)

        for t in range(TILES):
            j = near[TILES - 1 - t]
            if t == TILES - 1:
                halo_copy(sweep).wait_recv()
                came = halo_in[sweep].astype(F32).reshape(SIDE, CYCLE, frames).astype(BF16)

                @pl.when(tile == 0)
                def _():
                    win[sweep, :, TILES, CYCLE:EDGE] = came

                @pl.when(tile != 0)
                def _():
                    win[sweep, :, 0, 0:CYCLE] = came

            for b in range(TILES):
                first = b * EDGE - CYCLE
                low, high = max(first, 0), min(first + SPAN, SIDE)
                seen = win[sweep, low:high, pl.ds(j, 2)].reshape((high - low) * SPAN, frames)
                taken = band[j, b, :, (low - first) * SPAN : (high - first) * SPAN]
                back = jnp.dot(taken, seen, preferred_element_type=F32).astype(BF16)
                back = back.reshape(EDGE, EDGE, frames)
                rows = slice(b * EDGE, (b + 1) * EDGE)
                if sweep == PASSES - 1:
                    backs[j, rows] = back
                errs[j, rows] = (pm[j, rows] + back.astype(F32)).astype(BF16)

        grad = lax.dot_general(
            foot[...].reshape(pixels, comps),
            errs[...].reshape(pixels, frames),
            (((0,), (0,)), ((), ())),
            preferred_element_type=F32,
        )
        for q in range(frames // LANES):
            cols = slice(q * LANES, (q + 1) * LANES)
            moved = jnp.maximum(trace[:, cols].astype(F32) - grad[:, cols] * inv_den[...], 0.0)
            trace[:, cols] = jnp.where(live, moved, 0.0).astype(BF16)

    trace_copy = pltpu.make_async_copy(trace, new_trace, out_sems.at[0])
    trace_copy.start()
    squares = jnp.zeros((comps, LANES), F32)
    for q in range(frames // LANES):
        now = trace[:, q * LANES : (q + 1) * LANES].astype(F32)
        squares = squares + now * now
    energy = jnp.sum(jnp.transpose(squares), axis=0, keepdims=True)
    energy_out[...] = jnp.broadcast_to(energy, energy_out.shape)

    def energy_copy(peer, sender):
        return pltpu.make_async_remote_copy(
            src_ref=energy_out,
            dst_ref=energy_in.at[sender],
            send_sem=energy_sems.at[0, peer],
            recv_sem=energy_sems.at[1, sender],
            device_id={"tm": peer},
            device_id_type=MESH,
        )

    def part_copy(peer, sender):
        return pltpu.make_async_remote_copy(
            src_ref=part.at[peer],
            dst_ref=arrived.at[sender],
            send_sem=part_sems.at[0, peer],
            recv_sem=part_sems.at[1, sender],
            device_id={"tm": peer},
            device_id_type=MESH,
        )

    def gather_copy(peer, sender):
        return pltpu.make_async_remote_copy(
            src_ref=gathered.at[sender],
            dst_ref=gathered.at[sender],
            send_sem=gather_sems.at[0, peer],
            recv_sem=gather_sems.at[1, sender],
            device_id={"tm": peer},
            device_id_type=MESH,
        )

    def owns(index, do):
        if shares == n:
            do()
        else:
            pl.when(index < shares)(do)

    def over_peers(do):
        def step(t, carry):
            do(lax.rem(me + 1 + t, n))
            return carry

        lax.fori_loop(0, n - 1, step, 0)

    over_peers(lambda peer: owns(peer, lambda: energy_copy(peer, me).start()))

    def rows_of(ref, share):
        found = []
        for j in range(TILES):
            first = share * s if j % 2 == 0 else lax.rem(share * s + SHIFT, FOLD_ROWS)
            for lap in range(SIDE // FOLD_ROWS):
                found.append(ref[j, pl.ds(first + lap * FOLD_ROWS, s)])
        found = jnp.concatenate(found, axis=0)
        return found.reshape(found.shape[0] * EDGE, ref.shape[3])

    def fold(values):
        return jnp.sum(values.reshape(-1, s * EDGE, comps), axis=0)

    def share_of(share):
        feet = rows_of(foot, share)
        prod = jnp.dot(feet, trace[...], preferred_element_type=F32)
        ferr = prod + rows_of(backs, share).astype(F32) - rows_of(movie, share).astype(F32)
        grad = lax.dot_general(
            ferr.astype(BF16), trace[...], (((1,), (1,)), ((), ())), preferred_element_type=F32
        )
        return fold(jnp.where(feet.astype(F32) > 0.0, grad, 0.0))

    def send_share(share):
        part[share] = share_of(share).astype(BF16)
        part_copy(share, me).start()

    over_peers(lambda peer: owns(peer, lambda: send_share(peer)))

    def settle():
        own[...] = share_of(me)
        energy_in[me] = energy_out[...]

        def take(peer):
            energy_copy(me, peer).wait_recv()
            part_copy(me, peer).wait_recv()
            own[...] += arrived[peer].astype(F32)
            energy_in[me] += energy_in[peer]

        over_peers(take)
        den_c = energy_in[me][:1] + RIDGE_TERM
        feet = fold(rows_of(foot, me).astype(F32))
        gathered[me] = jnp.maximum(feet - own[...] / den_c, 0.0).astype(BF16)
        over_peers(lambda peer: gather_copy(peer, me).start())

    owns(me, settle)
    over_peers(lambda peer: owns(peer, lambda: gather_copy(me, peer).wait_recv()))
    packed_copy = pltpu.make_async_copy(gathered.at[0:shares], packed, out_sems.at[1])
    packed_copy.start()

    for sweep in range(PASSES):
        halo_copy(sweep).wait_send()

    def drain(peer):
        owns(peer, lambda: energy_copy(peer, me).wait_send())
        owns(peer, lambda: part_copy(peer, me).wait_send())
        owns(me, lambda: gather_copy(peer, me).wait_send())

    over_peers(drain)
    trace_copy.wait()
    packed_copy.wait()


def unfold(
    s, packed_in, trace_in, row_in, col_in, reach_in, count,
    new_foot, new_trace,
    packed, trace, row_at, col_at, reach, values, feet, load_sems, foot_sems,
):
    comps = feet.shape[2]
    loads = [
        pltpu.make_async_copy(source, target, load_sems.at[index])
        for index, (source, target) in enumerate((
            (packed_in, packed), (trace_in, trace), (row_in, row_at), (col_in, col_at), (reach_in, reach),
        ))
    ]
    for copy in loads:
        copy.start()
    for index in (0, 2, 3, 4):
        loads[index].wait()
    live = lax.broadcasted_iota(jnp.int32, (1, comps), 1) < count[0]
    bound = jnp.where(live, reach[...] * reach[...], -1)
    for r in range(FOLD_ROWS):
        values[r] = packed[r // s, r % s * EDGE : (r % s + 1) * EDGE].astype(F32)
    loads[1].wait()
    trace_copy = pltpu.make_async_copy(trace, new_trace, load_sems.at[1])
    trace_copy.start()
    col_sq = []
    for j in range(TILES):
        gap = lax.broadcasted_iota(jnp.int32, (EDGE, comps), 0) + j * EDGE - col_at[...]
        col_sq.append(gap * gap)

    def row(r):
        row_gap = r - row_at[...]
        edge = bound - row_gap * row_gap
        for j in range(TILES):
            value = values[lax.rem(r + j % 2 * SHIFT, FOLD_ROWS)]
            feet[r, j * EDGE : (j + 1) * EDGE] = jnp.where(col_sq[j] <= edge, value, 0.0).astype(BF16)

    copies = []
    for b in range(TILES):
        def step(t, carry):
            for u in range(2):
                row(b * EDGE + t * 2 + u)
            return carry

        lax.fori_loop(0, EDGE // 2, step, 0)
        rows = slice(b * EDGE, (b + 1) * EDGE)
        copies.append(pltpu.make_async_copy(feet.at[rows], new_foot.at[rows], foot_sems.at[b]))
        copies[-1].start()
    for copy in copies:
        copy.wait()
    trace_copy.wait()


def shards(movie, cycle_weights, footprints, traces, centre_row, centre_col, radius, comp_count):
    n = lax.axis_size("tm")
    frames = movie.shape[2]
    comps = footprints.shape[2]
    taps = cycle_weights.shape[2]
    s = -(-FOLD_ROWS // n)
    while SHIFT % s:
        s += 1
    shares = FOLD_ROWS // s
    anyspace = pl.BlockSpec(memory_space=pl.ANY)
    smem = pl.BlockSpec(memory_space=pltpu.SMEM)
    dma = pltpu.SemaphoreType.DMA
    packed, trace = pl.pallas_call(
        functools.partial(kernel, n, s, shares),
        out_shape=(
            jax.ShapeDtypeStruct((shares, s * EDGE, comps), BF16),
            jax.ShapeDtypeStruct((comps, frames), BF16),
        ),
        in_specs=[anyspace] * 7 + [smem, anyspace],
        out_specs=(anyspace, anyspace),
        scratch_shapes=[
            pltpu.VMEM((TILES, SIDE, EDGE, frames), BF16),
            pltpu.VMEM((taps, SIDE * SIDE), BF16),
            pltpu.VMEM((TILES, SIDE, EDGE, comps), BF16),
            pltpu.VMEM((comps, frames), BF16),
            pltpu.VMEM((1, comps), jnp.int32),
            pltpu.VMEM((1, comps), jnp.int32),
            pltpu.VMEM((1, comps), jnp.int32),
            pltpu.VMEM((STEP, CHUNKS, EDGE, LANES), jnp.int32),
            pltpu.VMEM((SIDE, TILES, EDGE, LANES), F32),
            pltpu.VMEM((TILES, SIDE, EDGE, comps), BF16),
            pltpu.VMEM((TILES, TILES, EDGE * EDGE, SPAN * SPAN), BF16),
            pltpu.VMEM((TILES, SIDE, EDGE, frames), F32),
            pltpu.VMEM((PASSES, SIDE, TILES + 1, EDGE, frames), BF16),
            pltpu.VMEM((TILES, SIDE, EDGE, frames), BF16),
            pltpu.VMEM((TILES, SIDE, EDGE, frames), BF16),
            pltpu.VMEM((comps, LANES), F32),
            pltpu.VMEM((PASSES, SIDE * CYCLE, frames), BF16),
            pltpu.VMEM((PASSES, SIDE * CYCLE, frames), BF16),
            pltpu.VMEM((n, s * EDGE, comps), BF16),
            pltpu.VMEM((s * EDGE, comps), F32),
            pltpu.VMEM((n, s * EDGE, comps), BF16),
            pltpu.VMEM((8, comps), F32),
            pltpu.VMEM((n, 8, comps), F32),
            pltpu.VMEM((n, s * EDGE, comps), BF16),
            dma((2, TILES, TILES)),
            dma((6,)),
            dma((2, PASSES)),
            dma((2, n)),
            dma((2, n)),
            dma((2, n)),
            dma((2,)),
        ],
        compiler_params=pltpu.CompilerParams(
            collective_id=0, has_side_effects=True, vmem_limit_bytes=60 * 1024 * 1024
        ),
    )(
        movie.reshape(SIDE, SIDE, frames),
        jnp.transpose(cycle_weights[0]),
        footprints.reshape(SIDE, SIDE, comps),
        traces.reshape(comps, frames),
        centre_row,
        centre_col,
        radius,
        comp_count,
        jnp.asarray(tap_tables()),
    )
    new_foot, new_trace = pl.pallas_call(
        functools.partial(unfold, s),
        out_shape=(
            jax.ShapeDtypeStruct((SIDE, SIDE, comps), BF16),
            jax.ShapeDtypeStruct((comps, frames), BF16),
        ),
        in_specs=[anyspace] * 5 + [smem],
        out_specs=(anyspace, anyspace),
        scratch_shapes=[
            pltpu.VMEM((shares, s * EDGE, comps), BF16),
            pltpu.VMEM((comps, frames), BF16),
            pltpu.VMEM((1, comps), jnp.int32),
            pltpu.VMEM((1, comps), jnp.int32),
            pltpu.VMEM((1, comps), jnp.int32),
            pltpu.VMEM((FOLD_ROWS, EDGE, comps), F32),
            pltpu.VMEM((SIDE, SIDE, comps), BF16),
            dma((5,)),
            dma((TILES,)),
        ],
    )(packed, trace, centre_row, centre_col, radius, comp_count)
    return (new_foot.reshape(1, SIDE * SIDE, comps), new_trace[None])


def solution(mesh):
    in_specs = (
        P(("groups", "tile"), None, "tm"),
        P(("groups", "tile"), None, None),
        P(("groups", "tile"), None, None),
        P(("groups", "tile"), None, "tm"),
        P(("groups", "tile"), None),
        P(("groups", "tile"), None),
        P(("groups", "tile"), None),
        P(("groups", "tile")),
    )
    out_specs = (P(("groups", "tile"), None, None), P(("groups", "tile"), None, "tm"))
    return jax.shard_map(shards, mesh=mesh, in_specs=in_specs, out_specs=out_specs, check_vma=False)
```

time: 49.6 us -> 41.6 us (0.84)
  Pallas kernels: 44.5 us -> 40 us
  local copies, waits for them, and re-layouts: 3.66 us -> 0 us
    pallas_call x1, Pallas kernels: 44.5 us -> 37.4 us  [shards(): pl.pallas_call(functools.partial(kernel, n, s, shares), out_shape=(jax.Sh...]
    unnamed x4 -> x0, local copies, waits for them, and re-layouts: 3.66 us -> none
    pallas_call x0 -> x1, Pallas kernels: none -> 2.55 us  [shards(): pl.pallas_call(functools.partial(unfold, s), out_shape=(jax.ShapeDtypeStr...]
where the time goes in v1:
time: 41.6 us; the launch traced here: 41.3 us
  Pallas kernels  40 us (96%)
  between operations  1.29 us (3%)
    pallas_call x1, Pallas kernels, shards(): pl.pallas_call(functools.partial(kernel, n, s, shares), out_shape=(jax.Sh...  37.4 us
    pallas_call x1, Pallas kernels, shards(): pl.pallas_call(functools.partial(unfold, s), out_shape=(jax.ShapeDtypeStr...  2.55 us

profile of v1, /device:TPU:0, one launch (start us, length us, event | category | flops | bytes accessed | tf_op | source)
XLA Modules:
  0.0 41.3 jit_solution(10070298726013428702)
XLA Ops:
  1.3 37.4 %shard_map.104 = (bf16[8,48,384]{2,1,0:T(8,128)(2,1)}, bf16[384,512]{1,0:T(8,128)(2,1)}) custom-call(bf16[48,48,512]{2,1,0:T(8,128)(2,1)} %bitcast.8, bf16[56,2304]{1,0:T(8,128)(2,1)} %bitcast.11, bf16[48,48,384]{2,1,0:T(8,128)(2,1)} %bitcast.9, bf16[384,512]{1,0:T(8,128)(2,1)} %bitcast.10, s32[1,384]{1,0:T(1,128)} %row_in.3, s32[1,384]{1,0:T(1,128)} %col_in.3, ...), custom_call_target="tpu_custom_call" | custom-call | tf_op jit(solution)/shard_map/pallas_call | solution.py:421
  38.7 2.5 %shard_map.105 = (bf16[48,48,384]{2,1,0:T(8,128)(2,1)}, bf16[384,512]{1,0:T(8,128)(2,1)}) custom-call(bf16[8,48,384]{2,1,0:T(8,128)(2,1)} %get-tuple-element.6.packed_in, bf16[384,512]{1,0:T(8,128)(2,1)} %get-tuple-element.7.trace_in, s32[1,384]{1,0:T(1,128)} %row_in.3, s32[1,384]{1,0:T(1,128)} %col_in.3, s32[1,384]{1,0:T(1,128)} %reach_in.3, s32[1]{0:T(128)S(6)} %copy.11.count), custom_call_target="tpu_custom_call" | custom-call | tf_op jit(solution)/shard_map/pallas_call | solution.py:476

commit v2 on v1

--- a/solution.py
+++ b/solution.py
@@ -18,8 +18,10 @@
 LANES = 128
 STEP = LANES // SPAN
 CHUNKS = (STEP - 1 + 2 * CYCLE) // STEP + 1
-FOLD_ROWS = 24
-SHIFT = FOLD_ROWS // 2
+FOLD_ROWS = 19
+SHIFT = 9
+TEAM_ROWS = 4
+ORDER = -1
 F32 = jnp.float32
 BF16 = jnp.bfloat16
 MESH = pl.DeviceIdType.MESH
@@ -37,7 +39,7 @@
 
 def tap_tables():
     offsets = {step: index for index, step in enumerate(cycle_offsets())}
-    tables = np.full((STEP, CHUNKS, EDGE, LANES), len(offsets), np.int32)
+    tables = np.full((STEP, CHUNKS, EDGE, LANES), len(offsets), np.int16)
     for phase in range(STEP):
         for chunk in range(CHUNKS):
             for col in range(EDGE):
@@ -49,8 +51,47 @@
     return tables
 
 
+def share_bounds(n):
+    base, extra = divmod(FOLD_ROWS, n)
+    bounds = [0]
+    for index in range(n):
+        bounds.append(bounds[-1] + base + (index >= n - extra))
+    return bounds
+
+
+def share_teams(bounds):
+    teams, held = [], []
+    for share in range(len(bounds) - 1):
+        if bounds[share] < bounds[share + 1]:
+            held.append(share)
+        if held and bounds[share + 1] - bounds[held[0]] >= TEAM_ROWS:
+            teams.append(held)
+            held = []
+    return teams + [held] if held else teams
+
+
+def fold_runs(first, last):
+    runs = []
+    for j in range(TILES):
+        for lap in range(-TILES, TILES + 1):
+            moved = SHIFT * j + FOLD_ROWS * lap
+            low, high = max(first + moved, 0), min(last + moved, SIDE)
+            if low < high:
+                runs.append((j, low, high, low - moved))
+    return runs
+
+
+def pick(values, index):
+    numbers = lax.GatherDimensionNumbers(
+        offset_dims=(), collapsed_slice_dims=(1,), start_index_map=(1,),
+        operand_batching_dims=(0,), start_indices_batching_dims=(0,),
+    )
+    inside = lax.GatherScatterMode.PROMISE_IN_BOUNDS
+    return lax.gather(values, index[..., None], numbers, (1, 1), mode=inside)
+
+
 def kernel(
-    n, s, shares,
+    n, bounds,
     movie_in, stored_in, prints_in, traces_in, row_in, col_in, reach_in, count, tables_in,
     packed, new_trace,
     movie, stored, prints, trace, row_at, col_at, reach, tables,
@@ -109,13 +150,6 @@
         cols = slice(q * LANES, (q + 1) * LANES)
         trace[:, cols] = jnp.where(live, trace[:, cols].astype(F32), 0.0).astype(BF16)
 
-    taps = stored.shape[0]
-    run = CYCLE * SIDE
-    for b in range(SIDE // CYCLE):
-        values = stored[:, b * run : (b + 1) * run].astype(F32)
-        values = jnp.concatenate([values, jnp.zeros((LANES - taps, run), F32)], axis=0)
-        weights[b * CYCLE : (b + 1) * CYCLE] = jnp.transpose(values).reshape(CYCLE, TILES, EDGE, LANES)
-
     col_sq = []
     for j in range(TILES):
         gap = lax.broadcasted_iota(jnp.int32, (EDGE, comps), 0) + j * EDGE - col_at[...]
@@ -139,14 +173,8 @@
                     total = total + kept * kept
                     held = weights[r, j]
                     for chunk in range(CHUNKS):
-                        found = [
-                            jnp.take_along_axis(
-                                held[h * 8 : h * 8 + 8], tables[phase, chunk, h * 8 : h * 8 + 8], axis=1
-                            )
-                            for h in range(EDGE // 8)
-                        ]
                         lane = pl.multiple_of((q + chunk) * LANES, LANES)
-                        band[j, b, pl.ds(spot, EDGE), pl.ds(lane, LANES)] = jnp.concatenate(found, axis=0).astype(BF16)
+                        band[j, b, pl.ds(spot, EDGE), pl.ds(lane, LANES)] = pick(held, tables[phase, chunk])
                     for chunk in range(CHUNKS, SPAN // STEP):
                         lane = pl.multiple_of(lax.rem(q + chunk, SPAN // STEP) * LANES, LANES)
                         band[j, b, pl.ds(spot, EDGE), pl.ds(lane, LANES)] = jnp.zeros((EDGE, LANES), BF16)
@@ -162,8 +190,15 @@
 
         return step
 
+    taps = stored.shape[0]
+    run = CYCLE * SIDE
     total = jnp.zeros((EDGE, comps), F32)
     for b in range(TILES):
+        for h in range(b * EDGE // CYCLE, (b + 1) * EDGE // CYCLE):
+            values = stored[:, h * run : (h + 1) * run].astype(F32)
+            values = jnp.concatenate([values, jnp.zeros((LANES - taps, run), F32)], axis=0)
+            turned = jnp.transpose(values).astype(BF16)
+            weights[h * CYCLE : (h + 1) * CYCLE] = turned.reshape(CYCLE, TILES, EDGE, LANES)
         for kind in range(2):
             for j in range(TILES):
                 load(b, j, kind).wait()
@@ -247,7 +282,7 @@
         now = trace[:, q * LANES : (q + 1) * LANES].astype(F32)
         squares = squares + now * now
     energy = jnp.sum(jnp.transpose(squares), axis=0, keepdims=True)
-    energy_out[...] = jnp.broadcast_to(energy, energy_out.shape)
+    energy_out[...] = energy
 
     def energy_copy(peer, sender):
         return pltpu.make_async_remote_copy(
@@ -259,31 +294,28 @@
             device_id_type=MESH,
         )
 
-    def part_copy(peer, sender):
+    def lines(share):
+        return slice(bounds[share] * EDGE, bounds[share + 1] * EDGE)
+
+    def part_copy(share, sender):
         return pltpu.make_async_remote_copy(
-            src_ref=part.at[peer],
-            dst_ref=arrived.at[sender],
-            send_sem=part_sems.at[0, peer],
+            src_ref=part.at[lines(share)],
+            dst_ref=arrived.at[sender, 0 : (bounds[share + 1] - bounds[share]) * EDGE],
+            send_sem=part_sems.at[0, share],
             recv_sem=part_sems.at[1, sender],
+            device_id={"tm": share},
+            device_id_type=MESH,
+        )
+
+    def gather_copy(peer, share):
+        return pltpu.make_async_remote_copy(
+            src_ref=gathered.at[lines(share)],
+            dst_ref=gathered.at[lines(share)],
+            send_sem=gather_sems.at[0, peer],
+            recv_sem=gather_sems.at[1, share],
             device_id={"tm": peer},
             device_id_type=MESH,
         )
-
-    def gather_copy(peer, sender):
-        return pltpu.make_async_remote_copy(
-            src_ref=gathered.at[sender],
-            dst_ref=gathered.at[sender],
-            send_sem=gather_sems.at[0, peer],
-            recv_sem=gather_sems.at[1, sender],
-            device_id={"tm": peer},
-            device_id_type=MESH,
-        )
-
-    def owns(index, do):
-        if shares == n:
-            do()
-        else:
-            pl.when(index < shares)(do)
 
     def over_peers(do):
         def step(t, carry):
@@ -292,71 +324,92 @@
 
         lax.fori_loop(0, n - 1, step, 0)
 
-    over_peers(lambda peer: owns(peer, lambda: energy_copy(peer, me).start()))
-
-    def rows_of(ref, share):
-        found = []
-        for j in range(TILES):
-            first = share * s if j % 2 == 0 else lax.rem(share * s + SHIFT, FOLD_ROWS)
-            for lap in range(SIDE // FOLD_ROWS):
-                found.append(ref[j, pl.ds(first + lap * FOLD_ROWS, s)])
-        found = jnp.concatenate(found, axis=0)
+    over_peers(lambda peer: energy_copy(peer, me).start())
+
+    def rows_of(ref, runs):
+        found = jnp.concatenate([ref[j, low:high] for j, low, high, _ in runs], axis=0)
         return found.reshape(found.shape[0] * EDGE, ref.shape[3])
 
-    def fold(values):
-        return jnp.sum(values.reshape(-1, s * EDGE, comps), axis=0)
-
-    def share_of(share):
-        feet = rows_of(foot, share)
+    def fold(values, runs, first, last):
+        values = values.reshape(-1, EDGE, comps)
+        totals, at = [None] * (last - first), 0
+        for _, low, high, row in runs:
+            for index in range(row - first, row - first + high - low):
+                totals[index] = values[at] if totals[index] is None else totals[index] + values[at]
+                at += 1
+        return totals
+
+    def grads_of(first, last):
+        runs = fold_runs(first, last)
+        feet = rows_of(foot, runs)
         prod = jnp.dot(feet, trace[...], preferred_element_type=F32)
-        ferr = prod + rows_of(backs, share).astype(F32) - rows_of(movie, share).astype(F32)
+        ferr = prod + rows_of(backs, runs).astype(F32) - rows_of(movie, runs).astype(F32)
         grad = lax.dot_general(
             ferr.astype(BF16), trace[...], (((1,), (1,)), ((), ())), preferred_element_type=F32
         )
-        return fold(jnp.where(feet.astype(F32) > 0.0, grad, 0.0))
-
-    def send_share(share):
-        part[share] = share_of(share).astype(BF16)
-        part_copy(share, me).start()
-
-    over_peers(lambda peer: owns(peer, lambda: send_share(peer)))
-
-    def settle():
-        own[...] = share_of(me)
-        energy_in[me] = energy_out[...]
+        return fold(jnp.where(feet.astype(F32) > 0.0, grad, 0.0), runs, first, last)
+
+    owned = [share for share in range(n) if bounds[share] < bounds[share + 1]]
+    teams = share_teams(bounds)
+    for team in teams[::ORDER]:
+        first, last = bounds[team[0]], bounds[team[-1] + 1]
+        found = grads_of(first, last)
+        for index in range(last - first):
+            part[(first + index) * EDGE : (first + index + 1) * EDGE] = found[index].astype(BF16)
+        for share in team:
+            @pl.when(me != share)
+            def _():
+                part_copy(share, me).start()
+
+            @pl.when(me == share)
+            def _():
+                for row in range(bounds[share], bounds[share + 1]):
+                    at = (row - bounds[share]) * EDGE
+                    own[at : at + EDGE] = found[row - first]
+
+    energy_in[me] = energy_out[...]
+
+    def take_energy(peer):
+        energy_copy(me, peer).wait_recv()
+        energy_in[me] += energy_in[peer]
+
+    over_peers(take_energy)
+    den_c = energy_in[me] + RIDGE_TERM
+
+    def settle(share):
+        first, last = bounds[share], bounds[share + 1]
+        size = (last - first) * EDGE
 
         def take(peer):
-            energy_copy(me, peer).wait_recv()
-            part_copy(me, peer).wait_recv()
-            own[...] += arrived[peer].astype(F32)
-            energy_in[me] += energy_in[peer]
+            part_copy(share, peer).wait_recv()
+            own[0:size] += arrived[peer, 0:size].astype(F32)
 
         over_peers(take)
-        den_c = energy_in[me][:1] + RIDGE_TERM
-        feet = fold(rows_of(foot, me).astype(F32))
-        gathered[me] = jnp.maximum(feet - own[...] / den_c, 0.0).astype(BF16)
-        over_peers(lambda peer: gather_copy(peer, me).start())
-
-    owns(me, settle)
-    over_peers(lambda peer: owns(peer, lambda: gather_copy(me, peer).wait_recv()))
-    packed_copy = pltpu.make_async_copy(gathered.at[0:shares], packed, out_sems.at[1])
+        runs = fold_runs(first, last)
+        feet = jnp.concatenate(fold(rows_of(foot, runs).astype(F32), runs, first, last), axis=0)
+        gathered[lines(share)] = jnp.maximum(feet - own[0:size] / den_c, 0.0).astype(BF16)
+        over_peers(lambda peer: gather_copy(peer, share).start())
+
+    for share in owned:
+        pl.when(me == share)(functools.partial(settle, share))
+    for share in owned[::ORDER]:
+        pl.when(me != share)(lambda: gather_copy(me, share).wait_recv())
+    packed_copy = pltpu.make_async_copy(gathered, packed, out_sems.at[1])
     packed_copy.start()
 
     for sweep in range(PASSES):
         halo_copy(sweep).wait_send()
 
-    def drain(peer):
-        owns(peer, lambda: energy_copy(peer, me).wait_send())
-        owns(peer, lambda: part_copy(peer, me).wait_send())
-        owns(me, lambda: gather_copy(peer, me).wait_send())
-
-    over_peers(drain)
+    over_peers(lambda peer: energy_copy(peer, me).wait_send())
+    for share in owned:
+        pl.when(me != share)(lambda: part_copy(share, me).wait_send())
+        pl.when(me == share)(lambda: over_peers(lambda peer: gather_copy(peer, share).wait_send()))
     trace_copy.wait()
     packed_copy.wait()
 
 
 def unfold(
-    s, packed_in, trace_in, row_in, col_in, reach_in, count,
+    packed_in, trace_in, row_in, col_in, reach_in, count,
     new_foot, new_trace,
     packed, trace, row_at, col_at, reach, values, feet, load_sems, foot_sems,
 ):
@@ -374,7 +427,7 @@
     live = lax.broadcasted_iota(jnp.int32, (1, comps), 1) < count[0]
     bound = jnp.where(live, reach[...] * reach[...], -1)
     for r in range(FOLD_ROWS):
-        values[r] = packed[r // s, r % s * EDGE : (r % s + 1) * EDGE].astype(F32)
+        values[r] = packed[r * EDGE : (r + 1) * EDGE].astype(F32)
     loads[1].wait()
     trace_copy = pltpu.make_async_copy(trace, new_trace, load_sems.at[1])
     trace_copy.start()
@@ -387,7 +440,7 @@
         row_gap = r - row_at[...]
         edge = bound - row_gap * row_gap
         for j in range(TILES):
-            value = values[lax.rem(r + j % 2 * SHIFT, FOLD_ROWS)]
+            value = values[lax.rem(r + (FOLD_ROWS - SHIFT) * j, FOLD_ROWS)]
             feet[r, j * EDGE : (j + 1) * EDGE] = jnp.where(col_sq[j] <= edge, value, 0.0).astype(BF16)
 
     copies = []
@@ -411,17 +464,15 @@
     frames = movie.shape[2]
     comps = footprints.shape[2]
     taps = cycle_weights.shape[2]
-    s = -(-FOLD_ROWS // n)
-    while SHIFT % s:
-        s += 1
-    shares = FOLD_ROWS // s
+    bounds = share_bounds(n)
+    widest = max(high - low for low, high in zip(bounds, bounds[1:])) * EDGE
     anyspace = pl.BlockSpec(memory_space=pl.ANY)
     smem = pl.BlockSpec(memory_space=pltpu.SMEM)
     dma = pltpu.SemaphoreType.DMA
     packed, trace = pl.pallas_call(
-        functools.partial(kernel, n, s, shares),
+        functools.partial(kernel, n, bounds),
         out_shape=(
-            jax.ShapeDtypeStruct((shares, s * EDGE, comps), BF16),
+            jax.ShapeDtypeStruct((FOLD_ROWS * EDGE, comps), BF16),
             jax.ShapeDtypeStruct((comps, frames), BF16),
         ),
         in_specs=[anyspace] * 7 + [smem, anyspace],
@@ -434,8 +485,8 @@
             pltpu.VMEM((1, comps), jnp.int32),
             pltpu.VMEM((1, comps), jnp.int32),
             pltpu.VMEM((1, comps), jnp.int32),
-            pltpu.VMEM((STEP, CHUNKS, EDGE, LANES), jnp.int32),
-            pltpu.VMEM((SIDE, TILES, EDGE, LANES), F32),
+            pltpu.VMEM((STEP, CHUNKS, EDGE, LANES), jnp.int16),
+            pltpu.VMEM((SIDE, TILES, EDGE, LANES), BF16),
             pltpu.VMEM((TILES, SIDE, EDGE, comps), BF16),
             pltpu.VMEM((TILES, TILES, EDGE * EDGE, SPAN * SPAN), BF16),
             pltpu.VMEM((TILES, SIDE, EDGE, frames), F32),
@@ -445,12 +496,12 @@
             pltpu.VMEM((comps, LANES), F32),
             pltpu.VMEM((PASSES, SIDE * CYCLE, frames), BF16),
             pltpu.VMEM((PASSES, SIDE * CYCLE, frames), BF16),
-            pltpu.VMEM((n, s * EDGE, comps), BF16),
-            pltpu.VMEM((s * EDGE, comps), F32),
-            pltpu.VMEM((n, s * EDGE, comps), BF16),
-            pltpu.VMEM((8, comps), F32),
-            pltpu.VMEM((n, 8, comps), F32),
-            pltpu.VMEM((n, s * EDGE, comps), BF16),
+            pltpu.VMEM((FOLD_ROWS * EDGE, comps), BF16),
+            pltpu.VMEM((widest, comps), F32),
+            pltpu.VMEM((n, widest, comps), BF16),
+            pltpu.VMEM((1, comps), F32),
+            pltpu.VMEM((n, 1, comps), F32),
+            pltpu.VMEM((FOLD_ROWS * EDGE, comps), BF16),
             dma((2, TILES, TILES)),
             dma((6,)),
             dma((2, PASSES)),
@@ -474,7 +525,7 @@
         jnp.asarray(tap_tables()),
     )
     new_foot, new_trace = pl.pallas_call(
-        functools.partial(unfold, s),
+        unfold,
         out_shape=(
             jax.ShapeDtypeStruct((SIDE, SIDE, comps), BF16),
             jax.ShapeDtypeStruct((comps, frames), BF16),
@@ -482,7 +533,7 @@
         in_specs=[anyspace] * 5 + [smem],
         out_specs=(anyspace, anyspace),
         scratch_shapes=[
-            pltpu.VMEM((shares, s * EDGE, comps), BF16),
+            pltpu.VMEM((FOLD_ROWS * EDGE, comps), BF16),
             pltpu.VMEM((comps, frames), BF16),
             pltpu.VMEM((1, comps), jnp.int32),
             pltpu.VMEM((1, comps), jnp.int32),

time: 41.6 us -> 38.7 us (0.930)
  Pallas kernels: 40 us -> 37.3 us
    pallas_call x2, Pallas kernels: 40 us -> 37.3 us  [the longest x1 34.6 us: shards(): pl.pallas_call(functools.partial(kernel, n, bounds), out_shape=(jax.Shape...]
where the time goes in v2:
time: 38.7 us; the launch traced here: 38.6 us
  Pallas kernels  37.3 us (96%)
  between operations  1.29 us (3%)
    pallas_call x1, Pallas kernels, shards(): pl.pallas_call(functools.partial(kernel, n, bounds), out_shape=(jax.Shape...  34.6 us
    pallas_call x1, Pallas kernels, shards(): pl.pallas_call(unfold, out_shape=(jax.ShapeDtypeStruct((SIDE, SIDE, comps...  2.71 us

profile of v2, /device:TPU:0, one launch (start us, length us, event | category | flops | bytes accessed | tf_op | source)
XLA Modules:
  0.0 38.6 jit_solution(14906161978628461704)
XLA Ops:
  1.3 34.6 %shard_map.104 = (bf16[304,384]{1,0:T(8,128)(2,1)}, bf16[384,512]{1,0:T(8,128)(2,1)}) custom-call(bf16[48,48,512]{2,1,0:T(8,128)(2,1)} %bitcast.8, bf16[56,2304]{1,0:T(8,128)(2,1)} %bitcast.11, bf16[48,48,384]{2,1,0:T(8,128)(2,1)} %bitcast.9, bf16[384,512]{1,0:T(8,128)(2,1)} %bitcast.10, s32[1,384]{1,0:T(1,128)} %row_in.3, s32[1,384]{1,0:T(1,128)} %col_in.3, ...), custom_call_target="tpu_custom_call" | custom-call | tf_op jit(solution)/shard_map/pallas_call | solution.py:472
  35.9 2.7 %shard_map.105 = (bf16[48,48,384]{2,1,0:T(8,128)(2,1)}, bf16[384,512]{1,0:T(8,128)(2,1)}) custom-call(bf16[304,384]{1,0:T(8,128)(2,1)} %get-tuple-element.6.packed_in, bf16[384,512]{1,0:T(8,128)(2,1)} %get-tuple-element.7.trace_in, s32[1,384]{1,0:T(1,128)} %row_in.3, s32[1,384]{1,0:T(1,128)} %col_in.3, s32[1,384]{1,0:T(1,128)} %reach_in.3, s32[1]{0:T(128)S(6)} %copy.11.count), custom_call_target="tpu_custom_call" | custom-call | tf_op jit(solution)/shard_map/pallas_call | solution.py:527

commit v3 on v2

--- a/solution.py
+++ b/solution.py
@@ -95,7 +95,7 @@
     movie_in, stored_in, prints_in, traces_in, row_in, col_in, reach_in, count, tables_in,
     packed, new_trace,
     movie, stored, prints, trace, row_at, col_at, reach, tables,
-    weights, foot, band, pm, win, errs, backs, inv_den,
+    weights, foot, band_first, band_second, band_third, pm, win, errs, backs, inv_den,
     halo_out, halo_in, part, own, arrived, energy_out, energy_in, gathered,
     load_sems, small_sems, halo_sems, part_sems, energy_sems, gather_sems, out_sems,
 ):
@@ -160,49 +160,66 @@
         win[sweep, rows, j, CYCLE:EDGE] = resid[:, 0:CYCLE]
         win[sweep, rows, j + 1, 0:CYCLE] = resid[:, CYCLE:EDGE]
 
-    def opening(b):
-        def step(q, total):
-            for phase in range(STEP):
-                r = b * EDGE + q * STEP + phase
-                spot = pl.multiple_of((q * STEP + phase) * EDGE, EDGE)
-                row_gap = r - row_at[...]
-                edge = bound - row_gap * row_gap
-                for j in range(TILES):
-                    kept = jnp.where(col_sq[j] <= edge, prints[j, r].astype(F32), 0.0)
-                    foot[j, r] = kept.astype(BF16)
-                    total = total + kept * kept
-                    held = weights[r, j]
-                    for chunk in range(CHUNKS):
-                        lane = pl.multiple_of((q + chunk) * LANES, LANES)
-                        band[j, b, pl.ds(spot, EDGE), pl.ds(lane, LANES)] = pick(held, tables[phase, chunk])
-                    for chunk in range(CHUNKS, SPAN // STEP):
-                        lane = pl.multiple_of(lax.rem(q + chunk, SPAN // STEP) * LANES, LANES)
-                        band[j, b, pl.ds(spot, EDGE), pl.ds(lane, LANES)] = jnp.zeros((EDGE, LANES), BF16)
-            rows = pl.ds(b * EDGE + q * STEP, STEP)
-            feet = foot[:, rows].reshape(TILES * STEP * EDGE, comps)
-            prod = jnp.dot(feet, trace[...], preferred_element_type=F32)
-            prod = prod.reshape(TILES, STEP, EDGE, frames)
+    near = [jnp.where(tile == 0, TILES - 1 - t, t) for t in range(TILES)]
+    bands = (band_first, band_second, band_third)
+
+    def weave(t, b, q, phase):
+        spot = (q * STEP + phase) * EDGE
+        held = weights[b * EDGE + q * STEP + phase, near[TILES - 1 - t]]
+        for chunk in range(SPAN // STEP):
+            if isinstance(q, int):
+                rows, lane = slice(spot, spot + EDGE), (q + chunk) % (SPAN // STEP) * LANES
+                lanes = slice(lane, lane + LANES)
+            else:
+                rows = pl.ds(pl.multiple_of(spot, EDGE), EDGE)
+                lane = q + chunk if chunk < CHUNKS else lax.rem(q + chunk, SPAN // STEP)
+                lanes = pl.ds(pl.multiple_of(lane * LANES, LANES), LANES)
+            if chunk < CHUNKS:
+                bands[t][b, rows, lanes] = pick(held, tables[phase, chunk])
+            else:
+                bands[t][b, rows, lanes] = jnp.zeros((EDGE, LANES), BF16)
+
+    def wait_for(kind, b):
+        for j in range(TILES):
+            load(b, j, kind).wait()
+
+    def mask_rows(b, total):
+        for r in range(b * EDGE, (b + 1) * EDGE):
+            row_gap = r - row_at[...]
+            edge = bound - row_gap * row_gap
             for j in range(TILES):
-                diff = prod[j] - movie[j, rows].astype(F32)
-                pm[j, rows] = diff
-                store_window(0, rows, j, diff)
-            return total
-
-        return step
+                kept = jnp.where(col_sq[j] <= edge, prints[j, r].astype(F32), 0.0)
+                foot[j, r] = kept.astype(BF16)
+                total = total + kept * kept
+        return total
+
+    def first_residual(b):
+        rows = slice(b * EDGE, (b + 1) * EDGE)
+        feet = foot[:, rows].reshape(TILES * EDGE * EDGE, comps)
+        prod = jnp.dot(feet, trace[...], preferred_element_type=F32)
+        prod = prod.reshape(TILES, EDGE, EDGE, frames)
+        for j in range(TILES):
+            diff = prod[j] - movie[j, rows].astype(F32)
+            pm[j, rows] = diff
+            store_window(0, rows, j, diff)
 
     taps = stored.shape[0]
     run = CYCLE * SIDE
-    total = jnp.zeros((EDGE, comps), F32)
+    for h in range(SIDE // CYCLE):
+        values = stored[:, h * run : (h + 1) * run].astype(F32)
+        values = jnp.concatenate([values, jnp.zeros((LANES - taps, run), F32)], axis=0)
+        turned = jnp.transpose(values).astype(BF16)
+        weights[h * CYCLE : (h + 1) * CYCLE] = turned.reshape(CYCLE, TILES, EDGE, LANES)
+    wait_for(0, 0)
+    total = mask_rows(0, jnp.zeros((EDGE, comps), F32))
     for b in range(TILES):
-        for h in range(b * EDGE // CYCLE, (b + 1) * EDGE // CYCLE):
-            values = stored[:, h * run : (h + 1) * run].astype(F32)
-            values = jnp.concatenate([values, jnp.zeros((LANES - taps, run), F32)], axis=0)
-            turned = jnp.transpose(values).astype(BF16)
-            weights[h * CYCLE : (h + 1) * CYCLE] = turned.reshape(CYCLE, TILES, EDGE, LANES)
-        for kind in range(2):
-            for j in range(TILES):
-                load(b, j, kind).wait()
-        total = lax.fori_loop(0, EDGE // STEP, opening(b), total)
+        wait_for(1, b)
+        if b + 1 < TILES:
+            wait_for(0, b + 1)
+            total = mask_rows(b + 1, total)
+        first_residual(b)
+        for i in range(EDGE):
+            weave(0, b, i // STEP, i % STEP)
     den = jnp.sum(total, axis=0, keepdims=True) + RIDGE_TERM
     inv_den[...] = jnp.transpose(jnp.broadcast_to(1.0 / den, (LANES, comps)))
 
@@ -221,7 +238,6 @@
         halo_out[sweep] = (-cut).reshape(SIDE * CYCLE, frames).astype(BF16)
         halo_copy(sweep).start()
 
-    near = [jnp.where(tile == 0, TILES - 1 - t, t) for t in range(TILES)]
     for sweep in range(PASSES):
         if sweep == 0:
             pl.semaphore_wait(barrier, n)
@@ -253,10 +269,13 @@
                     win[sweep, :, 0, 0:CYCLE] = came
 
             for b in range(TILES):
+                if sweep == 0 and t + 1 < TILES:
+                    for i in range(EDGE):
+                        weave(t + 1, b, i // STEP, i % STEP)
                 first = b * EDGE - CYCLE
                 low, high = max(first, 0), min(first + SPAN, SIDE)
                 seen = win[sweep, low:high, pl.ds(j, 2)].reshape((high - low) * SPAN, frames)
-                taken = band[j, b, :, (low - first) * SPAN : (high - first) * SPAN]
+                taken = bands[t][b, :, (low - first) * SPAN : (high - first) * SPAN]
                 back = jnp.dot(taken, seen, preferred_element_type=F32).astype(BF16)
                 back = back.reshape(EDGE, EDGE, frames)
                 rows = slice(b * EDGE, (b + 1) * EDGE)
@@ -444,14 +463,14 @@
             feet[r, j * EDGE : (j + 1) * EDGE] = jnp.where(col_sq[j] <= edge, value, 0.0).astype(BF16)
 
     copies = []
-    for b in range(TILES):
+    for b in range(SIDE // CYCLE):
         def step(t, carry):
-            for u in range(2):
-                row(b * EDGE + t * 2 + u)
+            for u in range(4):
+                row(b * CYCLE + t * 4 + u)
             return carry
 
-        lax.fori_loop(0, EDGE // 2, step, 0)
-        rows = slice(b * EDGE, (b + 1) * EDGE)
+        lax.fori_loop(0, CYCLE // 4, step, 0)
+        rows = slice(b * CYCLE, (b + 1) * CYCLE)
         copies.append(pltpu.make_async_copy(feet.at[rows], new_foot.at[rows], foot_sems.at[b]))
         copies[-1].start()
     for copy in copies:
@@ -488,7 +507,9 @@
             pltpu.VMEM((STEP, CHUNKS, EDGE, LANES), jnp.int16),
             pltpu.VMEM((SIDE, TILES, EDGE, LANES), BF16),
             pltpu.VMEM((TILES, SIDE, EDGE, comps), BF16),
-            pltpu.VMEM((TILES, TILES, EDGE * EDGE, SPAN * SPAN), BF16),
+            pltpu.VMEM((TILES, EDGE * EDGE, SPAN * SPAN), BF16),
+            pltpu.VMEM((TILES, EDGE * EDGE, SPAN * SPAN), BF16),
+            pltpu.VMEM((TILES, EDGE * EDGE, SPAN * SPAN), BF16),
             pltpu.VMEM((TILES, SIDE, EDGE, frames), F32),
             pltpu.VMEM((PASSES, SIDE, TILES + 1, EDGE, frames), BF16),
             pltpu.VMEM((TILES, SIDE, EDGE, frames), BF16),
@@ -541,7 +562,7 @@
             pltpu.VMEM((FOLD_ROWS, EDGE, comps), F32),
             pltpu.VMEM((SIDE, SIDE, comps), BF16),
             dma((5,)),
-            dma((TILES,)),
+            dma((SIDE // CYCLE,)),
         ],
     )(packed, trace, centre_row, centre_col, radius, comp_count)
     return (new_foot.reshape(1, SIDE * SIDE, comps), new_trace[None])

time: 38.7 us -> 36.7 us (0.948)
  Pallas kernels: 37.3 us -> 35.3 us
    pallas_call x1, Pallas kernels: 34.6 us -> 32.7 us  [shards(): pl.pallas_call(functools.partial(kernel, n, bounds), out_shape=(jax.Shape...]
where the time goes in v3:
time: 36.7 us; the launch traced here: 36.5 us
  Pallas kernels  35.3 us (96%)
  between operations  1.29 us (4%)
    pallas_call x1, Pallas kernels, shards(): pl.pallas_call(functools.partial(kernel, n, bounds), out_shape=(jax.Shape...  32.7 us
    pallas_call x1, Pallas kernels, shards(): pl.pallas_call(unfold, out_shape=(jax.ShapeDtypeStruct((SIDE, SIDE, comps...  2.55 us

profile of v3, /device:TPU:0, one launch (start us, length us, event | category | flops | bytes accessed | tf_op | source)
XLA Modules:
  0.0 36.5 jit_solution(6554251968524938889)
XLA Ops:
  1.3 32.7 %shard_map.104 = (bf16[304,384]{1,0:T(8,128)(2,1)}, bf16[384,512]{1,0:T(8,128)(2,1)}) custom-call(bf16[48,48,512]{2,1,0:T(8,128)(2,1)} %bitcast.8, bf16[56,2304]{1,0:T(8,128)(2,1)} %bitcast.11, bf16[48,48,384]{2,1,0:T(8,128)(2,1)} %bitcast.9, bf16[384,512]{1,0:T(8,128)(2,1)} %bitcast.10, s32[1,384]{1,0:T(1,128)} %row_in.3, s32[1,384]{1,0:T(1,128)} %col_in.3, ...), custom_call_target="tpu_custom_call" | custom-call | tf_op jit(solution)/shard_map/pallas_call | solution.py:491
  34.0 2.5 %shard_map.105 = (bf16[48,48,384]{2,1,0:T(8,128)(2,1)}, bf16[384,512]{1,0:T(8,128)(2,1)}) custom-call(bf16[304,384]{1,0:T(8,128)(2,1)} %get-tuple-element.6.packed_in, bf16[384,512]{1,0:T(8,128)(2,1)} %get-tuple-element.7.trace_in, s32[1,384]{1,0:T(1,128)} %row_in.3, s32[1,384]{1,0:T(1,128)} %col_in.3, s32[1,384]{1,0:T(1,128)} %reach_in.3, s32[1]{0:T(128)S(6)} %copy.11.count), custom_call_target="tpu_custom_call" | custom-call | tf_op jit(solution)/shard_map/pallas_call | solution.py:548

commit v4 on v3

--- a/solution.py
+++ b/solution.py
@@ -97,7 +97,7 @@
     movie, stored, prints, trace, row_at, col_at, reach, tables,
     weights, foot, band_first, band_second, band_third, pm, win, errs, backs, inv_den,
     halo_out, halo_in, part, own, arrived, energy_out, energy_in, gathered,
-    load_sems, small_sems, halo_sems, part_sems, energy_sems, gather_sems, out_sems,
+    load_sems, small_sems, halo_sems, part_sems, energy_sems, gather_sems,
 ):
     me = lax.axis_index("tm")
     tile = lax.axis_index("tile")
@@ -294,8 +294,7 @@
             moved = jnp.maximum(trace[:, cols].astype(F32) - grad[:, cols] * inv_den[...], 0.0)
             trace[:, cols] = jnp.where(live, moved, 0.0).astype(BF16)
 
-    trace_copy = pltpu.make_async_copy(trace, new_trace, out_sems.at[0])
-    trace_copy.start()
+    new_trace[...] = trace[...]
     squares = jnp.zeros((comps, LANES), F32)
     for q in range(frames // LANES):
         now = trace[:, q * LANES : (q + 1) * LANES].astype(F32)
@@ -413,8 +412,7 @@
         pl.when(me == share)(functools.partial(settle, share))
     for share in owned[::ORDER]:
         pl.when(me != share)(lambda: gather_copy(me, share).wait_recv())
-    packed_copy = pltpu.make_async_copy(gathered, packed, out_sems.at[1])
-    packed_copy.start()
+        packed[lines(share)] = gathered[lines(share)]
 
     for sweep in range(PASSES):
         halo_copy(sweep).wait_send()
@@ -423,33 +421,28 @@
     for share in owned:
         pl.when(me != share)(lambda: part_copy(share, me).wait_send())
         pl.when(me == share)(lambda: over_peers(lambda peer: gather_copy(peer, share).wait_send()))
-    trace_copy.wait()
-    packed_copy.wait()
 
 
 def unfold(
-    packed_in, trace_in, row_in, col_in, reach_in, count,
+    packed, trace, row_in, col_in, reach_in, count,
     new_foot, new_trace,
-    packed, trace, row_at, col_at, reach, values, feet, load_sems, foot_sems,
+    row_at, col_at, reach, values, feet, load_sems, foot_sems,
 ):
     comps = feet.shape[2]
     loads = [
         pltpu.make_async_copy(source, target, load_sems.at[index])
         for index, (source, target) in enumerate((
-            (packed_in, packed), (trace_in, trace), (row_in, row_at), (col_in, col_at), (reach_in, reach),
+            (trace, new_trace), (row_in, row_at), (col_in, col_at), (reach_in, reach),
         ))
     ]
     for copy in loads:
         copy.start()
-    for index in (0, 2, 3, 4):
-        loads[index].wait()
+    for copy in loads[1:]:
+        copy.wait()
     live = lax.broadcasted_iota(jnp.int32, (1, comps), 1) < count[0]
     bound = jnp.where(live, reach[...] * reach[...], -1)
     for r in range(FOLD_ROWS):
         values[r] = packed[r * EDGE : (r + 1) * EDGE].astype(F32)
-    loads[1].wait()
-    trace_copy = pltpu.make_async_copy(trace, new_trace, load_sems.at[1])
-    trace_copy.start()
     col_sq = []
     for j in range(TILES):
         gap = lax.broadcasted_iota(jnp.int32, (EDGE, comps), 0) + j * EDGE - col_at[...]
@@ -475,7 +468,7 @@
         copies[-1].start()
     for copy in copies:
         copy.wait()
-    trace_copy.wait()
+    loads[0].wait()
 
 
 def shards(movie, cycle_weights, footprints, traces, centre_row, centre_col, radius, comp_count):
@@ -491,11 +484,11 @@
     packed, trace = pl.pallas_call(
         functools.partial(kernel, n, bounds),
         out_shape=(
-            jax.ShapeDtypeStruct((FOLD_ROWS * EDGE, comps), BF16),
-            jax.ShapeDtypeStruct((comps, frames), BF16),
+            pltpu.VMEM((FOLD_ROWS * EDGE, comps), BF16),
+            pltpu.VMEM((comps, frames), BF16),
         ),
         in_specs=[anyspace] * 7 + [smem, anyspace],
-        out_specs=(anyspace, anyspace),
+        out_specs=(pl.BlockSpec(memory_space=pltpu.VMEM), pl.BlockSpec(memory_space=pltpu.VMEM)),
         scratch_shapes=[
             pltpu.VMEM((TILES, SIDE, EDGE, frames), BF16),
             pltpu.VMEM((taps, SIDE * SIDE), BF16),
@@ -529,10 +522,9 @@
             dma((2, n)),
             dma((2, n)),
             dma((2, n)),
-            dma((2,)),
         ],
         compiler_params=pltpu.CompilerParams(
-            collective_id=0, has_side_effects=True, vmem_limit_bytes=60 * 1024 * 1024
+            collective_id=0, has_side_effects=True, vmem_limit_bytes=62600000
         ),
     )(
         movie.reshape(SIDE, SIDE, frames),
@@ -551,19 +543,18 @@
             jax.ShapeDtypeStruct((SIDE, SIDE, comps), BF16),
             jax.ShapeDtypeStruct((comps, frames), BF16),
         ),
-        in_specs=[anyspace] * 5 + [smem],
+        in_specs=[pl.BlockSpec(memory_space=pltpu.VMEM)] * 2 + [anyspace] * 3 + [smem],
         out_specs=(anyspace, anyspace),
         scratch_shapes=[
-            pltpu.VMEM((FOLD_ROWS * EDGE, comps), BF16),
-            pltpu.VMEM((comps, frames), BF16),
             pltpu.VMEM((1, comps), jnp.int32),
             pltpu.VMEM((1, comps), jnp.int32),
             pltpu.VMEM((1, comps), jnp.int32),
             pltpu.VMEM((FOLD_ROWS, EDGE, comps), F32),
             pltpu.VMEM((SIDE, SIDE, comps), BF16),
-            dma((5,)),
+            dma((4,)),
             dma((SIDE // CYCLE,)),
         ],
+        compiler_params=pltpu.CompilerParams(vmem_limit_bytes=12 * 1024 * 1024),
     )(packed, trace, centre_row, centre_col, radius, comp_count)
     return (new_foot.reshape(1, SIDE * SIDE, comps), new_trace[None])
 

time: 36.7 us -> 35.2 us (0.959)
  Pallas kernels: 35.3 us -> 33.7 us
    pallas_call x1, Pallas kernels: 2.55 us -> 1.43 us  [shards(): pl.pallas_call(unfold, out_shape=(jax.ShapeDtypeStruct((SIDE, SIDE, comps...]
    pallas_call x1, Pallas kernels: 32.7 us -> 32.3 us  [shards(): pl.pallas_call(functools.partial(kernel, n, bounds), out_shape=(pltpu.VME...]
where the time goes in v4:
time: 35.2 us; the launch traced here: 35 us
  Pallas kernels  33.7 us (96%)
  between operations  1.33 us (4%)
    pallas_call x1, Pallas kernels, shards(): pl.pallas_call(functools.partial(kernel, n, bounds), out_shape=(pltpu.VME...  32.3 us
    pallas_call x1, Pallas kernels, shards(): pl.pallas_call(unfold, out_shape=(jax.ShapeDtypeStruct((SIDE, SIDE, comps...  1.43 us

profile of v4, /device:TPU:0, one launch (start us, length us, event | category | flops | bytes accessed | tf_op | source)
XLA Modules:
  0.0 35.0 jit_solution(11525004741671195155)
XLA Ops:
  1.3 0.0 copy-start
  1.3 0.0 copy-start.1
  1.3 0.0 copy-start.2
  1.3 32.3 %shard_map.104 = (bf16[304,384]{1,0:T(8,128)(2,1)S(1)}, bf16[384,512]{1,0:T(8,128)(2,1)S(1)}) custom-call(bf16[48,48,512]{2,1,0:T(8,128)(2,1)} %bitcast.8, bf16[56,2304]{1,0:T(8,128)(2,1)} %bitcast.11, bf16[48,48,384]{2,1,0:T(8,128)(2,1)} %bitcast.9, bf16[384,512]{1,0:T(8,128)(2,1)} %bitcast.10, s32[1,384]{1,0:T(1,128)} %row_in.3, s32[1,384]{1,0:T(1,128)} %col_in.3, ...), custom_call_target="tpu_custom_call" | custom-call | tf_op jit(solution)/shard_map/pallas_call | solution.py:484
  33.6 0.0 copy-done
  33.6 0.0 copy-done.1
  33.6 0.0 copy-done.2
  33.6 1.4 %shard_map.105 = (bf16[48,48,384]{2,1,0:T(8,128)(2,1)}, bf16[384,512]{1,0:T(8,128)(2,1)}) custom-call(bf16[304,384]{1,0:T(8,128)(2,1)S(1)} %get-tuple-element.6.packed, bf16[384,512]{1,0:T(8,128)(2,1)S(1)} %get-tuple-element.7.trace, s32[1,384]{1,0:T(1,128)S(1)} %copy-done, s32[1,384]{1,0:T(1,128)S(1)} %copy-done.1, s32[1,384]{1,0:T(1,128)S(1)} %copy-done.2, ...), custom_call_target="tpu_custom_call" | custom-call | tf_op jit(solution)/shard_map/pallas_call | solution.py:540
Async XLA Ops:
  1.3 32.3 %copy-start = (s32[1,384]{1,0:T(1,128)S(1)}, s32[1,384]{1,0:T(1,128)}, u32[]{:S(2)}) copy-start(s32[1,384]{1,0:T(1,128)} %row_in.3) | copy-start | bytes 4612
  1.3 32.3 %copy-start.1 = (s32[1,384]{1,0:T(1,128)S(1)}, s32[1,384]{1,0:T(1,128)}, u32[]{:S(2)}) copy-start(s32[1,384]{1,0:T(1,128)} %col_in.3) | copy-start | bytes 4612
  1.3 32.3 %copy-start.2 = (s32[1,384]{1,0:T(1,128)S(1)}, s32[1,384]{1,0:T(1,128)}, u32[]{:S(2)}) copy-start(s32[1,384]{1,0:T(1,128)} %reach_in.3) | copy-start | bytes 4612

commit v5 on v4

--- a/solution.py
+++ b/solution.py
@@ -369,7 +369,7 @@
 
     owned = [share for share in range(n) if bounds[share] < bounds[share + 1]]
     teams = share_teams(bounds)
-    for team in teams[::ORDER]:
+    for team in teams[-2:] + teams[-3::-1]:
         first, last = bounds[team[0]], bounds[team[-1] + 1]
         found = grads_of(first, last)
         for index in range(last - first):

time: 35.2 us -> 33.8 us (0.960)
  Pallas kernels: 33.7 us -> 32.3 us
    pallas_call x1, Pallas kernels: 32.3 us -> 30.9 us  [shards(): pl.pallas_call(functools.partial(kernel, n, bounds), out_shape=(pltpu.VME...]
where the time goes in v5:
time: 33.8 us; the launch traced here: 33.7 us
  Pallas kernels  32.3 us (96%)
  between operations  1.33 us (4%)
    pallas_call x1, Pallas kernels, shards(): pl.pallas_call(functools.partial(kernel, n, bounds), out_shape=(pltpu.VME...  30.9 us
    pallas_call x1, Pallas kernels, shards(): pl.pallas_call(unfold, out_shape=(jax.ShapeDtypeStruct((SIDE, SIDE, comps...  1.43 us

profile of v5, /device:TPU:0, one launch (start us, length us, event | category | flops | bytes accessed | tf_op | source)
XLA Modules:
  0.0 33.7 jit_solution(15065387792219234347)
XLA Ops:
  1.3 0.0 copy-start
  1.3 0.0 copy-start.1
  1.3 0.0 copy-start.2
  1.3 30.9 %shard_map.104 = (bf16[304,384]{1,0:T(8,128)(2,1)S(1)}, bf16[384,512]{1,0:T(8,128)(2,1)S(1)}) custom-call(bf16[48,48,512]{2,1,0:T(8,128)(2,1)} %bitcast.8, bf16[56,2304]{1,0:T(8,128)(2,1)} %bitcast.11, bf16[48,48,384]{2,1,0:T(8,128)(2,1)} %bitcast.9, bf16[384,512]{1,0:T(8,128)(2,1)} %bitcast.10, s32[1,384]{1,0:T(1,128)} %row_in.3, s32[1,384]{1,0:T(1,128)} %col_in.3, ...), custom_call_target="tpu_custom_call" | custom-call | tf_op jit(solution)/shard_map/pallas_call | solution.py:484
  32.2 0.0 copy-done
  32.2 0.0 copy-done.1
  32.2 0.0 copy-done.2
  32.2 1.4 %shard_map.105 = (bf16[48,48,384]{2,1,0:T(8,128)(2,1)}, bf16[384,512]{1,0:T(8,128)(2,1)}) custom-call(bf16[304,384]{1,0:T(8,128)(2,1)S(1)} %get-tuple-element.6.packed, bf16[384,512]{1,0:T(8,128)(2,1)S(1)} %get-tuple-element.7.trace, s32[1,384]{1,0:T(1,128)S(1)} %copy-done, s32[1,384]{1,0:T(1,128)S(1)} %copy-done.1, s32[1,384]{1,0:T(1,128)S(1)} %copy-done.2, ...), custom_call_target="tpu_custom_call" | custom-call | tf_op jit(solution)/shard_map/pallas_call | solution.py:540
Async XLA Ops:
  1.3 30.9 %copy-start = (s32[1,384]{1,0:T(1,128)S(1)}, s32[1,384]{1,0:T(1,128)}, u32[]{:S(2)}) copy-start(s32[1,384]{1,0:T(1,128)} %row_in.3) | copy-start | bytes 4612
  1.3 30.9 %copy-start.1 = (s32[1,384]{1,0:T(1,128)S(1)}, s32[1,384]{1,0:T(1,128)}, u32[]{:S(2)}) copy-start(s32[1,384]{1,0:T(1,128)} %col_in.3) | copy-start | bytes 4612
  1.3 30.9 %copy-start.2 = (s32[1,384]{1,0:T(1,128)S(1)}, s32[1,384]{1,0:T(1,128)}, u32[]{:S(2)}) copy-start(s32[1,384]{1,0:T(1,128)} %reach_in.3) | copy-start | bytes 4612
